TPU v7x, 128 devices: a whole 4x4x4 slice. The times are simulated.
128 devices in a mesh: ga: 16 (over x, z_hi, core), ba: 8 (over y, z_lo).
Axes of the slice: x: 4, y: 4, z: 4 (z_hi: 2, z_lo: 2; z = z_hi * 2 + z_lo), core: 2. Of those that a mesh axis runs over, the one named last changes fastest.
Arguments:
- psi: float32 [2, 32768, 2048], P(None, 'ga', 'ba'), may hold values from -0.15625 to 0.15625
- dpsi: float32 [2, 32768, 512], P(None, 'ga', 'ba'), may hold values from -6 to 6
- band_weight: float32 [2048], replicated, may hold values from 0.25 to 1
- panel_band: int32 [16], P('ba'), may hold values from 0 to 15, each once
- slab_offset: int32 [16], replicated, may hold values from 0 to 2047
Outputs:
- projected: float32 [2, 32768, 512], P(None, 'ga', 'ba')
Inputs may be any that keep to these rules, and one draw needn't show every extreme that they name: panel_band is a permutation of the panel numbers.
All inputs are finite; a program needn't handle non-finite values.
Results may differ from a plain program's by a relative error of at most 0.00012.
Values sent between devices are 32-bit elements; how exact they have to be, the bound alone decides.
A program may use at most 128 MiB of HBM per device.

v0:
```python
import jax
import jax.numpy as jnp
from jax import lax
from jax.sharding import PartitionSpec as P

PANEL = 128


def split_up(value, dim, count):
    before, after = (value.shape[:dim], value.shape[dim + 1 :])
    return jnp.moveaxis(value.reshape(*before, count, -1, *after), dim, 0)


def edges_of(length, count):
    turn = length // count
    if turn >= 8:
        turn -= turn % 8
    return [turn * k for k in range(1, count)]


def in_order(blocks, dim):
    lengths = list(blocks.shape[1:])
    lengths[dim] *= blocks.shape[0]
    return jnp.moveaxis(blocks, 0, dim).reshape(lengths)


def cut_exchange(value, axis, pieces, split_dim, concat_dim):
    blocks = split_up(value, split_dim, lax.axis_size(axis))
    split_at = max(range(1, max(2, blocks.ndim - 1)), key=lambda d: blocks.shape[d])
    done = []
    for slab in jnp.split(blocks, edges_of(blocks.shape[split_at], pieces), axis=split_at):
        if slab.size:
            done.append(lax.all_to_all(slab, axis, split_axis=0, concat_axis=0, tiled=True))
    return in_order(jnp.concatenate(done, axis=split_at), concat_dim)


def from_everyone(value, axis):
    count = lax.axis_size(axis)
    return lax.all_to_all(
        jnp.broadcast_to(value[None], (count, *value.shape)), axis, 0, 0, tiled=True
    )


def gather_directly(value, axis, dim):
    blocks = from_everyone(value, axis)
    return in_order(blocks, dim)


def tdot(left, right):
    return lax.dot_general(
        left,
        right,
        (((0,), (0,)), ((), ())),
        precision=lax.Precision.HIGHEST,
        preferred_element_type=jnp.float32,
    )


def mdot(left, right):
    return jnp.dot(left, right, precision=lax.Precision.HIGHEST, preferred_element_type=jnp.float32)


def margin_of(waves, columns):
    over_re = tdot(waves[0], columns[0]) + tdot(waves[1], columns[1])
    over_im = tdot(waves[0], columns[1]) - tdot(waves[1], columns[0])
    return jnp.stack([over_re, over_im])


def correct_with(waves, weighted):
    corr_re = mdot(waves[0], weighted[0]) - mdot(waves[1], weighted[1])
    corr_im = mdot(waves[0], weighted[1]) + mdot(waves[1], weighted[0])
    return jnp.stack([corr_re, corr_im])


def weights_for(band_weight, panels):
    table = band_weight.reshape(-1, PANEL)
    onehot = (panels[:, None] == jnp.arange(table.shape[0], dtype=jnp.int32)[None, :]).astype(
        jnp.float32
    )
    return mdot(onehot, table).reshape(-1)


def per_device(psi, dpsi, band_weight, panel_band, slab_offset):
    offset = slab_offset[lax.axis_index("ga")]
    aligned = jnp.roll(dpsi, -offset, axis=1)
    row_waves, row_columns = (
        cut_exchange(psi, "ba", 2, 1, 2),
        cut_exchange(aligned, "ba", 2, 1, 2),
    )
    all_panels = gather_directly(panel_band, "ba", 0)
    full_weight = weights_for(band_weight, all_panels)
    margin = lax.psum(margin_of(row_waves, row_columns), ("ga", "ba"))
    weighted = margin * full_weight[None, :, None]
    row_result = row_columns - correct_with(row_waves, weighted)
    result = lax.all_to_all(row_result, "ba", split_axis=2, concat_axis=1, tiled=True)
    return jnp.roll(result, offset, axis=1)


def solution(mesh):
    in_specs = (P(None, "ga", "ba"), P(None, "ga", "ba"), P(), P("ba"), P())
    out_specs = P(None, "ga", "ba")
    return jax.shard_map(
        per_device, mesh=mesh, in_specs=in_specs, out_specs=out_specs, check_vma=False
    )
```

profile of v0, /device:TPU:2, one launch (start us, length us, event | category | flops | bytes accessed | tf_op | source)
XLA Modules:
  0.0 354.8 jit_solution(3534208202760883374)
XLA Ops:
  12.1 5.8 %all-to-all-start.1 = ((f32[8,2,128,64]{2,3,1,0:T(8,128)}), f32[8,2,128,64]{2,3,1,0:T(8,128)S(1)}, u32[]{:S(2)}, u32[]{:S(2)}) async-start(f32[8,2,128,64]{2,3,1,0:T(8,128)} %copy.21), calls=%async_computation.1 | async-start | bytes 1048576 | tf_op jit(solution)/shard_map/all_to_all | solution.py:33
  18.8 8.7 %all-to-all-done.1 = f32[8,2,128,64]{2,3,1,0:T(8,128)S(1)} async-done(((f32[8,2,128,64]{2,3,1,0:T(8,128)}), f32[8,2,128,64]{2,3,1,0:T(8,128)S(1)}, u32[]{:S(2)}, u32[]{:S(2)}) %all-to-all-start.1) | async-done | bytes 524320 | tf_op jit(solution)/shard_map/all_to_all | solution.py:33
  27.5 3.5 all-to-all-start
  31.0 4.0 %fusion.13 = (f32[8,2,128,256]{3,2,0,1:T(8,128)}, f32[8,2,128,256]{3,2,0,1:T(8,128)S(1)}) fusion(f32[8,2,256,256]{3,2,0,1:T(8,128)} %bitcast.83), kind=kLoop, calls=%fused_computation.29 | loop fusion | bytes 8388608 | tf_op jit(solution)/shard_map/split | solution.py:31
  36.5 3.4 all-to-all-done
  39.9 3.6 %all-to-all-start.3 = ((f32[8,2,128,256]{3,2,1,0:T(8,128)}), f32[8,2,128,256]{3,2,1,0:T(8,128)S(1)}, u32[]{:S(2)}, u32[]{:S(2)}) async-start(f32[8,2,128,256]{3,2,1,0:T(8,128)} %copy.25), calls=%async_computation.3 | async-start | bytes 4194304 | tf_op jit(solution)/shard_map/all_to_all | solution.py:33
  46.6 26.9 %all-to-all-done.3 = f32[8,2,128,256]{3,2,1,0:T(8,128)S(1)} async-done(((f32[8,2,128,256]{3,2,1,0:T(8,128)}), f32[8,2,128,256]{3,2,1,0:T(8,128)S(1)}, u32[]{:S(2)}, u32[]{:S(2)}) %all-to-all-start.3) | async-done | bytes 2097184 | tf_op jit(solution)/shard_map/all_to_all | solution.py:33
  73.5 4.3 %all-to-all-start.2 = ((f32[8,2,128,256]{3,2,1,0:T(8,128)}), f32[8,2,128,256]{3,2,1,0:T(8,128)}, u32[]{:S(2)}, u32[]{:S(2)}) async-start(f32[8,2,128,256]{3,2,1,0:T(8,128)} %copy.24), calls=%async_computation.2 | async-start | bytes 4194304 | tf_op jit(solution)/shard_map/all_to_all | solution.py:33
  81.0 26.4 %all-to-all-done.2 = f32[8,2,128,256]{3,2,1,0:T(8,128)} async-done(((f32[8,2,128,256]{3,2,1,0:T(8,128)}), f32[8,2,128,256]{3,2,1,0:T(8,128)}, u32[]{:S(2)}, u32[]{:S(2)}) %all-to-all-start.2) | async-done | bytes 2097184 | tf_op jit(solution)/shard_map/all_to_all | solution.py:33
  107.4 3.3 copy.26
  113.2 3.7 %fusion.17 = f32[2048,512]{1,0:T(8,128)S(1)} fusion(f32[256,2048]{0,1:T(8,128)S(1)} %bitcast.68, f32[256,512]{0,1:T(8,128)S(1)} %bitcast.76), kind=kOutput, calls=%fused_computation.33 | convolution fusion | flops 3221225472 | bytes 6815744 | tf_op jit(solution)/shard_map/dot_general | solution.py:50
  116.9 3.7 %fusion.16 = f32[2048,512]{1,0:T(8,128)S(1)} fusion(f32[256,2048]{0,1:T(8,128)S(1)} %bitcast.69, f32[256,512]{0,1:T(8,128)S(1)} %bitcast.78), kind=kOutput, calls=%fused_computation.32 | convolution fusion | flops 3221225472 | bytes 6815744 | tf_op jit(solution)/shard_map/dot_general | solution.py:50
  120.7 3.8 %subtract_bitcast_fusion = f32[1,2048,512]{2,1,0:T(8,128)S(1)} fusion(f32[2048,512]{1,0:T(8,128)S(1)} %fusion.17, f32[256,2048]{0,1:T(8,128)S(1)} %bitcast.72, f32[256,512]{0,1:T(8,128)S(1)} %bitcast.79), kind=kOutput, calls=%fused_computation.5 | convolution fusion | flops 3222274048 | bytes 11010048 | tf_op jit(solution)/shard_map/dot_general | solution.py:50
  124.4 15.3 %add_bitcast_fusion = f32[1,2048,512]{2,1,0:T(8,128)S(1)} fusion(f32[2048,512]{1,0:T(8,128)S(1)} %fusion.16, f32[256,2048]{0,1:T(8,128)S(1)} %bitcast.73, f32[256,512]{0,1:T(8,128)S(1)} %bitcast.77), kind=kOutput, calls=%fused_computation.6 | convolution fusion | flops 3222274048 | bytes 11010048 | tf_op jit(solution)/shard_map/dot_general | solution.py:50
  139.7 4.2 %pad_maximum_fusion = f32[2,2048,512]{2,1,0:T(8,128)} fusion(f32[1,2048,512]{2,1,0:T(8,128)S(1)} %subtract_bitcast_fusion, f32[1,2048,512]{2,1,0:T(8,128)S(1)} %add_bitcast_fusion), kind=kLoop, calls=%fused_computation | loop fusion | flops 2097152 | bytes 16777216 | tf_op jit(solution)/shard_map/stack | solution.py:66
  144.6 8.5 %all_to_all.44 = s32[8,1,2]{2,1,0:T(1,128)S(1)} all-to-all(s32[8,1,2]{2,1,0:T(1,128)S(1)} %broadcast_in_dim.2), channel_id=1, replica_groups=mesh['ga'=16,'ba'=8] {'ba'}, dimensions={0} | all-to-all | bytes 128 | tf_op jit(solution)/shard_map/all_to_all | solution.py:39
  156.0 148.4 %all-reduce.2.cloned.1.call-done = f32[2,2048,512]{2,1,0:T(8,128)} async-done(((f32[2,2048,512]{2,1,0:T(8,128)}), f32[2,2048,512]{2,1,0:T(8,128)}) %all-reduce.2.cloned.1.call-update) | async-done | bytes 8388624 | tf_op jit(solution)/shard_map/psum | solution.py:92
  304.4 4.1 %broadcast_multiply_fusion = f32[2,2048,512]{2,1,0:T(8,128)S(1)} fusion(f32[2,2048,512]{2,1,0:T(8,128)} %all-reduce.2.cloned.1.call-done, f32[2048]{0:T(1024)S(1)} %convolution_bitcast_fusion), kind=kLoop, calls=%fused_computation.4 | loop fusion | flops 2097152 | bytes 16785408 | tf_op jit(solution)/shard_map/mul | solution.py:93
  308.6 3.8 %fusion = f32[256,512]{1,0:T(8,128)S(1)} fusion(f32[256,2048]{0,1:T(8,128)S(1)} %bitcast.74, f32[2,2048,512]{2,1,0:T(8,128)S(1)} %broadcast_multiply_fusion), kind=kOutput, calls=%fused_computation.7 | convolution fusion | flops 3221225472 | bytes 6815744 | tf_op jit(solution)/shard_map/dot_general | solution.py:60
  312.4 3.9 %fusion.1 = f32[256,512]{1,0:T(8,128)S(1)} fusion(f32[256,2048]{0,1:T(8,128)S(1)} %bitcast.70, f32[2,2048,512]{2,1,0:T(8,128)S(1)} %broadcast_multiply_fusion), kind=kOutput, calls=%fused_computation.8 | convolution fusion | flops 3221225472 | bytes 6815744 | tf_op jit(solution)/shard_map/dot_general | solution.py:60
  316.3 4.1 %fusion.7 = f32[1,256,512]{2,1,0:T(8,128)S(1)} fusion(f32[256,512]{1,0:T(8,128)S(1)} %fusion, f32[256,2048]{0,1:T(8,128)S(1)} %bitcast.71, f32[2,2048,512]{2,1,0:T(8,128)S(1)} %broadcast_multiply_fusion), kind=kOutput, calls=%fused_computation.18 | convolution fusion | flops 3221356544 | bytes 7340032 | tf_op jit(solution)/shard_map/dot_general | solution.py:60
  320.4 3.8 %fusion.5 = f32[1,256,512]{2,1,0:T(8,128)S(1)} fusion(f32[256,512]{1,0:T(8,128)S(1)} %fusion.1, f32[256,2048]{0,1:T(8,128)S(1)} %bitcast.75, f32[2,2048,512]{2,1,0:T(8,128)S(1)} %broadcast_multiply_fusion), kind=kOutput, calls=%fused_computation.16 | convolution fusion | flops 3221356544 | bytes 7340032 | tf_op jit(solution)/shard_map/dot_general | solution.py:60
  325.7 3.6 %all-to-all-start.5 = ((f32[2,256,512]{1,0,2:T(2,128)}), f32[2,256,512]{1,0,2:T(2,128)S(1)}, u32[]{:S(2)}, u32[]{:S(2)}) async-start(f32[2,256,512]{1,0,2:T(2,128)} %copy.29), calls=%async_computation.5 | async-start | bytes 2097152 | tf_op jit(solution)/shard_map/all_to_all | solution.py:95
  330.5 15.5 %all-to-all-done.5 = f32[2,256,512]{1,0,2:T(2,128)S(1)} async-done(((f32[2,256,512]{1,0,2:T(2,128)}), f32[2,256,512]{1,0,2:T(2,128)S(1)}, u32[]{:S(2)}, u32[]{:S(2)}) %all-to-all-start.5) | async-done | bytes 1048608 | tf_op jit(solution)/shard_map/all_to_all | solution.py:95
  (40 shorter events, 22.4 us)
Async XLA Ops:
  6.5 148.0 %copy-start = (f32[2048]{0:T(1024)S(1)}, f32[2048]{0:T(1024)}, u32[]{:S(2)}) copy-start(f32[2048]{0:T(1024)} %param.9) | copy-start | bytes 24580
  12.1 15.4 %all-to-all-start.1 = ((f32[8,2,128,64]{2,3,1,0:T(8,128)}), f32[8,2,128,64]{2,3,1,0:T(8,128)S(1)}, u32[]{:S(2)}, u32[]{:S(2)}) async-start(f32[8,2,128,64]{2,3,1,0:T(8,128)} %copy.21), calls=%async_computation.1 | async-start | bytes 1048576 | tf_op jit(solution)/shard_map/all_to_all | solution.py:33
  27.5 12.4 %all-to-all-start = ((f32[8,2,128,64]{2,3,1,0:T(8,128)}), f32[8,2,128,64]{2,3,1,0:T(8,128)S(1)}, u32[]{:S(2)}, u32[]{:S(2)}) async-start(f32[8,2,128,64]{2,3,1,0:T(8,128)} %copy.20), calls=%async_computation | async-start | bytes 1048576 | tf_op jit(solution)/shard_map/all_to_all | solution.py:33
  39.9 33.6 %all-to-all-start.3 = ((f32[8,2,128,256]{3,2,1,0:T(8,128)}), f32[8,2,128,256]{3,2,1,0:T(8,128)S(1)}, u32[]{:S(2)}, u32[]{:S(2)}) async-start(f32[8,2,128,256]{3,2,1,0:T(8,128)} %copy.25), calls=%async_computation.3 | async-start | bytes 4194304 | tf_op jit(solution)/shard_map/all_to_all | solution.py:33
  73.5 33.9 %all-to-all-start.2 = ((f32[8,2,128,256]{3,2,1,0:T(8,128)}), f32[8,2,128,256]{3,2,1,0:T(8,128)}, u32[]{:S(2)}, u32[]{:S(2)}) async-start(f32[8,2,128,256]{3,2,1,0:T(8,128)} %copy.24), calls=%async_computation.2 | async-start | bytes 4194304 | tf_op jit(solution)/shard_map/all_to_all | solution.py:33
  77.8 226.6 %all-reduce.2.cloned.1.call-start = ((), (), s32[]{:S(2)}) async-start(), calls=%async_computation.6 | async-start | bytes 16777216 | tf_op jit(solution)/shard_map/psum | solution.py:92
  81.0 29.7 %copy-start.3 = (f32[8,2,128,256]{2,3,0,1:T(8,128)S(1)}, f32[8,2,128,256]{2,3,0,1:T(8,128)}, u32[]{:S(2)}) copy-start(f32[8,2,128,256]{2,3,0,1:T(8,128)} %copy.27) | copy-start | bytes 6291460
  113.2 11.2 %copy-start.1 = (f32[1,256,8,256]{1,3,2,0:T(8,128)}, f32[1,256,8,256]{1,3,2,0:T(8,128)S(1)}, u32[]{:S(2)}) copy-start(f32[1,256,8,256]{1,3,2,0:T(8,128)S(1)} %get-tuple-element.7) | copy-start | bytes 6291460
  143.9 0.7 copy-start.6
  143.9 10.8 %copy-start.4 = (f32[8,2,256,64]{2,3,0,1:T(8,128)S(1)}, f32[8,2,256,64]{2,3,0,1:T(8,128)}, u32[]{:S(2)}) copy-start(f32[8,2,256,64]{2,3,0,1:T(8,128)} %get-tuple-element.13) | copy-start | bytes 3145732
  304.4 4.1 %copy-start.2 = (f32[1,256,8,256]{1,3,2,0:T(8,128)S(1)}, f32[1,256,8,256]{1,3,2,0:T(8,128)}, u32[]{:S(2)}) copy-start(f32[1,256,8,256]{1,3,2,0:T(8,128)} %copy-done.1) | copy-start | bytes 6291460
  320.3 3.9 %copy-start.5 = (f32[2,256,512]{2,1,0:T(8,128)S(1)}, f32[2,256,512]{2,1,0:T(8,128)}, u32[]{:S(2)}) copy-start(f32[2,256,512]{2,1,0:T(8,128)} %copy.28) | copy-start | bytes 3145732
  325.7 20.3 %all-to-all-start.5 = ((f32[2,256,512]{1,0,2:T(2,128)}), f32[2,256,512]{1,0,2:T(2,128)S(1)}, u32[]{:S(2)}, u32[]{:S(2)}) async-start(f32[2,256,512]{1,0,2:T(2,128)} %copy.29), calls=%async_computation.5 | async-start | bytes 2097152 | tf_op jit(solution)/shard_map/all_to_all | solution.py:95
Sparse Core Ops, SparseCore 0:
  144.1 160.2 all-reduce.1
where the time goes:
time: 359 us; the launch traced here: 355 us
  waiting for transfers between devices  229 us (64%)
  matrix products  42.2 us (12%)
  local copies, waits for them, and re-layouts  21.8 us (6%)
  starting transfers between devices  20.9 us (6%)
  between operations  16.2 us (5%)
  other arithmetic  15.9 us (4%)
  blocking collectives  8.52 us (2%)
    psum x1, waiting for transfers between devices, per_device(): margin = lax.psum(margin_of(row_waves, row_columns), ('ga', 'ba'))  148 us
    all_to_all x4, waiting for transfers between devices, cut_exchange(): lax.all_to_all(slab, axis, split_axis=0, concat_axis=0, tiled=True)  65.3 us
    dot_general x4, matrix products, tdot(): lax.dot_general(left, right, (((0,), (0,)), ((), ())), precision=lax.Prec...  26.5 us
    all_to_all x4, starting transfers between devices, cut_exchange(): lax.all_to_all(slab, axis, split_axis=0, concat_axis=0, tiled=True)  17.3 us
    dot_general x5, matrix products, mdot(): jnp.dot(left, right, precision=lax.Precision.HIGHEST, preferred_element_t...  15.8 us
    all_to_all x1, waiting for transfers between devices, per_device(): lax.all_to_all(row_result, 'ba', split_axis=2, concat_axis=1, tiled=True)  15.5 us
    split x6, local copies, waits for them, and re-layouts, cut_exchange(): jnp.split(blocks, edges_of(blocks.shape[split_at], pieces), axis=split_at)  10.5 us
    all_to_all x1, blocking collectives, from_everyone(): lax.all_to_all(jnp.broadcast_to(value[None], (count, *value.shape)), axis...  8.52 us
  transfers between devices with their start and end apart: 6, of which 6 were waited for; matrix products, arithmetic and copies ran while one was open for 4% of the time, Pallas kernels for 0%

commit v1 on v0

--- a/solution.py
+++ b/solution.py
@@ -89,7 +89,9 @@
     )
     all_panels = gather_directly(panel_band, "ba", 0)
     full_weight = weights_for(band_weight, all_panels)
-    margin = lax.psum(margin_of(row_waves, row_columns), ("ga", "ba"))
+    margin = margin_of(row_waves, row_columns)
+    for mesh_axis in ("ba", "ga"):
+        margin = lax.psum(margin, mesh_axis)
     weighted = margin * full_weight[None, :, None]
     row_result = row_columns - correct_with(row_waves, weighted)
     result = lax.all_to_all(row_result, "ba", split_axis=2, concat_axis=1, tiled=True)

time: 359 us -> 747 us (2.08)
  waiting for transfers between devices: 229 us -> 611 us
    psum x1 -> x2, waiting for transfers between devices: 148 us -> 529 us  [per_device(): margin = lax.psum(margin, mesh_axis)]
  transfers between devices with their start and end apart: 6 -> 7, of which waited for: 6 -> 7; matrix products, arithmetic and copies ran while one was open for 4% -> 2% of each run, Pallas kernels for 0% -> 0%
where the time goes in v1:
time: 747 us; the launch traced here: 743 us
  waiting for transfers between devices  611 us (82%)
  matrix products  42.3 us (6%)
  local copies, waits for them, and re-layouts  21.8 us (3%)
  starting transfers between devices  21.6 us (3%)
  between operations  16.2 us (2%)
  other arithmetic  15.9 us (2%)
  blocking collectives  14.1 us (2%)
    psum x2, waiting for transfers between devices, per_device(): margin = lax.psum(margin, mesh_axis)  529 us
    all_to_all x4, waiting for transfers between devices, cut_exchange(): lax.all_to_all(slab, axis, split_axis=0, concat_axis=0, tiled=True)  65.3 us
    dot_general x4, matrix products, tdot(): lax.dot_general(left, right, (((0,), (0,)), ((), ())), precision=lax.Prec...  26.5 us
    all_to_all x4, starting transfers between devices, cut_exchange(): lax.all_to_all(slab, axis, split_axis=0, concat_axis=0, tiled=True)  17.3 us
    all_to_all x1, waiting for transfers between devices, per_device(): lax.all_to_all(row_result, 'ba', split_axis=2, concat_axis=1, tiled=True)  16.3 us
    dot_general x5, matrix products, mdot(): jnp.dot(left, right, precision=lax.Precision.HIGHEST, preferred_element_t...  15.8 us
  transfers between devices with their start and end apart: 7, of which 7 were waited for; matrix products, arithmetic and copies ran while one was open for 2% of the time, Pallas kernels for 0%

profile of v1, /device:TPU:2, one launch (start us, length us, event | category | flops | bytes accessed | tf_op | source)
XLA Modules:
  0.0 742.8 jit_solution(13227554287532873247)
XLA Ops:
  12.1 5.8 all-to-all-start.1
  18.8 8.7 %all-to-all-done.1 = f32[8,2,128,64]{2,3,1,0:T(8,128)S(1)} async-done(((f32[8,2,128,64]{2,3,1,0:T(8,128)}), f32[8,2,128,64]{2,3,1,0:T(8,128)S(1)}, u32[]{:S(2)}, u32[]{:S(2)}) %all-to-all-start.1) | async-done | bytes 524320 | tf_op jit(solution)/shard_map/all_to_all | solution.py:33
  27.5 3.5 all-to-all-start
  31.0 4.0 fusion.13
  36.5 3.4 all-to-all-done
  39.9 3.6 all-to-all-start.3
  46.6 26.9 %all-to-all-done.3 = f32[8,2,128,256]{3,2,1,0:T(8,128)S(1)} async-done(((f32[8,2,128,256]{3,2,1,0:T(8,128)}), f32[8,2,128,256]{3,2,1,0:T(8,128)S(1)}, u32[]{:S(2)}, u32[]{:S(2)}) %all-to-all-start.3) | async-done | bytes 2097184 | tf_op jit(solution)/shard_map/all_to_all | solution.py:33
  73.5 4.3 all-to-all-start.2
  81.0 26.4 %all-to-all-done.2 = f32[8,2,128,256]{3,2,1,0:T(8,128)} async-done(((f32[8,2,128,256]{3,2,1,0:T(8,128)}), f32[8,2,128,256]{3,2,1,0:T(8,128)}, u32[]{:S(2)}, u32[]{:S(2)}) %all-to-all-start.2) | async-done | bytes 2097184 | tf_op jit(solution)/shard_map/all_to_all | solution.py:33
  113.2 3.7 fusion.17
  116.9 3.7 fusion.16
  120.7 3.8 subtract_bitcast_fusion
  124.4 15.3 %add_bitcast_fusion = f32[1,2048,512]{2,1,0:T(8,128)S(1)} fusion(f32[2048,512]{1,0:T(8,128)S(1)} %fusion.16, f32[256,2048]{0,1:T(8,128)S(1)} %bitcast.73, f32[256,512]{0,1:T(8,128)S(1)} %bitcast.77), kind=kOutput, calls=%fused_computation.6 | convolution fusion | flops 3222274048 | bytes 11010048 | tf_op jit(solution)/shard_map/dot_general | solution.py:50
  139.8 4.2 pad_maximum_fusion
  144.1 339.0 %all-reduce.3.cloned.1.call-done = f32[2,2048,512]{2,1,0:T(8,128)} async-done(((f32[2,2048,512]{2,1,0:T(8,128)}), f32[2,2048,512]{2,1,0:T(8,128)}) %all-reduce.3.cloned.1.call-update) | async-done | bytes 8388624 | tf_op jit(solution)/shard_map/psum | solution.py:94
  483.8 14.1 %all_to_all.44 = s32[8,1,2]{2,1,0:T(1,128)S(1)} all-to-all(s32[8,1,2]{2,1,0:T(1,128)S(1)} %broadcast_in_dim.2), channel_id=1, replica_groups=mesh['ga'=16,'ba'=8] {'ba'}, dimensions={0} | all-to-all | bytes 128 | tf_op jit(solution)/shard_map/all_to_all | solution.py:39
  500.8 190.2 %all-reduce.5.cloned.1.call-done = f32[2,2048,512]{2,1,0:T(8,128)} async-done(((f32[2,2048,512]{2,1,0:T(8,128)}), f32[2,2048,512]{2,1,0:T(8,128)}) %all-reduce.5.cloned.1.call-update) | async-done | bytes 8388624 | tf_op jit(solution)/shard_map/psum | solution.py:94
  690.9 4.1 broadcast_multiply_fusion
  695.1 3.8 fusion
  698.9 3.9 fusion.1
  702.8 4.1 fusion.7
  706.9 3.8 fusion.5
  712.2 4.3 all-to-all-start.5
  717.7 16.3 %all-to-all-done.5 = f32[2,256,512]{1,0,2:T(2,128)S(1)} async-done(((f32[2,256,512]{1,0,2:T(2,128)}), f32[2,256,512]{1,0,2:T(2,128)S(1)}, u32[]{:S(2)}, u32[]{:S(2)}) %all-to-all-start.5) | async-done | bytes 1048608 | tf_op jit(solution)/shard_map/all_to_all | solution.py:97
  (43 shorter events, 25.7 us)
Async XLA Ops:
  6.5 492.7 %copy-start = (f32[2048]{0:T(1024)S(1)}, f32[2048]{0:T(1024)}, u32[]{:S(2)}) copy-start(f32[2048]{0:T(1024)} %param.9) | copy-start | bytes 24580
  12.1 15.4 %all-to-all-start.1 = ((f32[8,2,128,64]{2,3,1,0:T(8,128)}), f32[8,2,128,64]{2,3,1,0:T(8,128)S(1)}, u32[]{:S(2)}, u32[]{:S(2)}) async-start(f32[8,2,128,64]{2,3,1,0:T(8,128)} %copy.21), calls=%async_computation.1 | async-start | bytes 1048576 | tf_op jit(solution)/shard_map/all_to_all | solution.py:33
  27.5 12.4 %all-to-all-start = ((f32[8,2,128,64]{2,3,1,0:T(8,128)}), f32[8,2,128,64]{2,3,1,0:T(8,128)S(1)}, u32[]{:S(2)}, u32[]{:S(2)}) async-start(f32[8,2,128,64]{2,3,1,0:T(8,128)} %copy.20), calls=%async_computation | async-start | bytes 1048576 | tf_op jit(solution)/shard_map/all_to_all | solution.py:33
  39.9 33.6 %all-to-all-start.3 = ((f32[8,2,128,256]{3,2,1,0:T(8,128)}), f32[8,2,128,256]{3,2,1,0:T(8,128)S(1)}, u32[]{:S(2)}, u32[]{:S(2)}) async-start(f32[8,2,128,256]{3,2,1,0:T(8,128)} %copy.25), calls=%async_computation.3 | async-start | bytes 4194304 | tf_op jit(solution)/shard_map/all_to_all | solution.py:33
  73.5 33.9 %all-to-all-start.2 = ((f32[8,2,128,256]{3,2,1,0:T(8,128)}), f32[8,2,128,256]{3,2,1,0:T(8,128)}, u32[]{:S(2)}, u32[]{:S(2)}) async-start(f32[8,2,128,256]{3,2,1,0:T(8,128)} %copy.24), calls=%async_computation.2 | async-start | bytes 4194304 | tf_op jit(solution)/shard_map/all_to_all | solution.py:33
  77.8 405.3 %all-reduce.3.cloned.1.call-start = ((), (), s32[]{:S(2)}) async-start(), calls=%async_computation.6 | async-start | bytes 16777216 | tf_op jit(solution)/shard_map/psum | solution.py:94
  81.0 29.7 %copy-start.3 = (f32[8,2,128,256]{2,3,0,1:T(8,128)S(1)}, f32[8,2,128,256]{2,3,0,1:T(8,128)}, u32[]{:S(2)}) copy-start(f32[8,2,128,256]{2,3,0,1:T(8,128)} %copy.27) | copy-start | bytes 6291460
  113.2 11.2 %copy-start.1 = (f32[1,256,8,256]{1,3,2,0:T(8,128)}, f32[1,256,8,256]{1,3,2,0:T(8,128)S(1)}, u32[]{:S(2)}) copy-start(f32[1,256,8,256]{1,3,2,0:T(8,128)S(1)} %get-tuple-element.7) | copy-start | bytes 6291460
  144.0 546.9 %all-reduce.5.cloned.1.call-start = ((), (), s32[]{:S(2)}) async-start(), calls=%async_computation.7 | async-start | bytes 16777216 | tf_op jit(solution)/shard_map/psum | solution.py:94
  483.1 0.7 copy-start.6
  483.1 16.3 %copy-start.4 = (f32[8,2,256,64]{2,3,0,1:T(8,128)S(1)}, f32[8,2,256,64]{2,3,0,1:T(8,128)}, u32[]{:S(2)}) copy-start(f32[8,2,256,64]{2,3,0,1:T(8,128)} %get-tuple-element.13) | copy-start | bytes 3145732
  690.9 4.1 copy-start.2
  706.8 3.9 copy-start.5
  712.2 21.7 %all-to-all-start.5 = ((f32[2,256,512]{1,0,2:T(2,128)}), f32[2,256,512]{1,0,2:T(2,128)S(1)}, u32[]{:S(2)}, u32[]{:S(2)}) async-start(f32[2,256,512]{1,0,2:T(2,128)} %copy.29), calls=%async_computation.5 | async-start | bytes 2097152 | tf_op jit(solution)/shard_map/all_to_all | solution.py:97
Sparse Core Ops, SparseCore 0:
  144.1 338.9 all-reduce.2
  485.6 205.2 all-reduce.4
